TPU v7x, 32 devices: a whole 2x2x4 slice. The times are simulated.
32 devices in a mesh: macro: 8 (over z, x), rep: 4 (over y, core).
Axes of the slice: x: 2, y: 2, z: 4, core: 2. Of those that a mesh axis runs over, the one named last changes fastest.
Arguments:
- u_old: float32 [4096], P('macro'), may hold values from -1 to 1
- coarse_kinetic_speed: float32 [4096], P('macro'), may hold values from 0.2 to 3
- micro_spreading_coefficient: float32 [4096], P('macro'), may hold values from 0.08 to 0.4
- micro_seed: int32 [4, 4096, 256], P('rep', 'macro'), may hold values from 0 to 1073741823
Outputs:
- new_state: float32 [4096], P('macro')
All inputs are finite; a program needn't handle non-finite values.
Results may differ from a plain program's by a relative error of at most 0.0001.
Values sent between devices are 32-bit elements; how exact they have to be, the bound alone decides.
A program may use at most 64 MiB of HBM per device.

v0:
```python
import math
import jax
import jax.numpy as jnp
from jax import lax
from jax.sharding import PartitionSpec as P

STEPS = 8
ITERS = 4
noise_amp = 1.0
micro_dt = 0.02
proj_step = 0.25
fd_step = 0.01
seed_scale = 2.0 ** (-30)


def with_halo(cells, sides, width):
    for axis, dim in sides:
        count = lax.axis_size(axis)
        ends = count - 1
        head = lax.slice_in_dim(cells, 0, width, axis=dim)
        tail = lax.slice_in_dim(cells, cells.shape[dim] - width, cells.shape[dim], axis=dim)
        cells = jnp.concatenate(
            [
                lax.ppermute(tail, axis, [(i, (i + 1) % count) for i in range(ends)]),
                cells,
                lax.ppermute(head, axis, [((i + 1) % count, i) for i in range(ends)]),
            ],
            axis=dim,
        )
    return cells


def lifted(padded_density, cells):
    left = padded_density[:-2]
    centre = padded_density[1:-1]
    right = padded_density[2:]
    slope = 0.5 * (right - left)
    bend = 0.5 * (right - 2.0 * centre + left)
    place = (jnp.arange(cells).astype(jnp.float32) + 0.5) / cells - 0.5
    inside = (
        centre[:, None] + slope[:, None] * place[None, :] + bend[:, None] * (place * place)[None, :]
    )
    edge = 0.5 + 0.5 / cells
    ghost_left = centre - slope * edge + bend * edge * edge
    ghost_right = centre + slope * edge + bend * edge * edge
    return (inside, ghost_left, ghost_right)


def ensemble_aggregate(padded_density, pointwise_kinetic_speed, spreading_current, stochastic_kick):
    inside, ghost_left, ghost_right = lifted(padded_density, stochastic_kick.shape[2])
    start = inside[None] + stochastic_kick
    left_col = ghost_left[None, :, None]
    right_col = ghost_right[None, :, None]
    kappa = spreading_current[None, :, None]
    growth = micro_dt * pointwise_kinetic_speed[None, :, None]
    state = start
    for step in range(STEPS):
        upper = jnp.concatenate([state[:, :, 1:], right_col], axis=2)
        lower = jnp.concatenate([left_col, state[:, :, :-1]], axis=2)
        state = (
            state + kappa * (upper + lower - 2.0 * state) + growth * (state - state * state * state)
        )
    return jnp.sum(state - start, axis=(0, 2))


def least_squares(hess, beta, iters):
    target = [beta] + [beta * 0.0 for index in range(iters)]
    cosines = []
    sines = []
    upper = []
    for col_index in range(iters):
        column = [hess[row][col_index] for row in range(col_index + 2)]
        for row in range(col_index):
            first = column[row]
            second = column[row + 1]
            column[row] = cosines[row] * first + sines[row] * second
            column[row + 1] = -sines[row] * first + cosines[row] * second
        radius = jnp.sqrt(
            column[col_index] * column[col_index] + column[col_index + 1] * column[col_index + 1]
        )
        cosine = column[col_index] / radius
        sine = column[col_index + 1] / radius
        cosines.append(cosine)
        sines.append(sine)
        column[col_index] = radius
        upper.append(column[: col_index + 1])
        head = target[col_index]
        target[col_index] = cosine * head
        target[col_index + 1] = -sine * head
    solved = [None] * iters
    for row in range(iters - 1, -1, -1):
        acc = target[row]
        for later in range(row + 1, iters):
            acc = acc - upper[later][row] * solved[later]
        solved[row] = acc / upper[row][row]
    return solved


def per_device(u_old, coarse_kinetic_speed, micro_spreading_coefficient, micro_seed):
    local = u_old.shape[0]
    groups = lax.axis_size("rep")
    fluctuation_amplitude = 1.0 / (
        micro_seed.shape[0] * groups * micro_seed.shape[2] * STEPS * micro_dt
    )
    delta = fd_step * math.sqrt(lax.axis_size("macro") * local)
    stochastic_kick = noise_amp * (micro_seed.astype(jnp.float32) * seed_scale - 0.5)

    def drift(species_density):
        padded_density = with_halo(species_density, (("macro", 0),), 1)
        increment_parts = ensemble_aggregate(
            padded_density, coarse_kinetic_speed, micro_spreading_coefficient, stochastic_kick
        )
        summed = lax.psum(increment_parts, "rep")
        return summed * fluctuation_amplitude

    def inner(values):
        return lax.psum(values, "macro")

    f_old = drift(u_old)
    u_start = u_old + proj_step * f_old
    f_start = drift(u_start)
    resid = -(u_start - u_old - proj_step * f_start)
    beta = jnp.sqrt(inner(jnp.sum(resid * resid)))
    basis = [resid / beta]
    hess = [[None] * ITERS for row in range(ITERS + 1)]
    for col_index in range(ITERS):
        probe = basis[col_index]
        image = probe - proj_step * (drift(u_start + delta * probe) - f_start) / delta
        pieces = [jnp.sum(basis[row] * image) for row in range(col_index + 1)]
        pieces.append(jnp.sum(image * image))
        dots = inner(jnp.stack(pieces))
        for row in range(col_index + 1):
            hess[row][col_index] = dots[row]
            image = image - dots[row] * basis[row]
        coeff_sq = jnp.sum(dots[: col_index + 1] * dots[: col_index + 1])
        length = jnp.sqrt(jnp.maximum(dots[col_index + 1] - coeff_sq, 0.0))
        hess[col_index + 1][col_index] = length
        basis.append(image / length)
    coeffs = least_squares(hess, beta, ITERS)
    result = u_start
    for col_index in range(ITERS):
        result = result + coeffs[col_index] * basis[col_index]
    return result


def solution(mesh):
    placed = (P("macro"), P("macro"), P("macro"), P("rep", "macro", None))
    return jax.shard_map(
        per_device, mesh=mesh, in_specs=placed, out_specs=P("macro"), check_vma=False
    )
```

profile of v0, /device:TPU:0, one launch (start us, length us, event | category | flops | bytes accessed | tf_op | source)
XLA Modules:
  0.0 276.7 jit_solution(14354860609766797719)
XLA Ops:
  0.0 1.4 fusion.354
  1.4 1.4 collective-permute-start
  2.8 6.0 %collective-permute-start.1 = (f32[1]{0:T(128)}, f32[1]{0:T(128)}, u32[]{:S(2)}, u32[]{:S(2)}) collective-permute-start(f32[1]{0:T(128)} %get-tuple-element.172), channel_id=1, source_target_pairs={{0,4},{4,8},{8,12},{12,16},{16,20},{20,24},{24,28},{1,5},{5,9},{9,... | collective-permute-start | bytes 20 | tf_op jit(solution)/shard_map/ppermute | solution.py:24
  9.7 1.3 pad_maximum_fusion.96
  11.0 1.3 add_add_fusion.5
  18.9 6.5 %psum.77 = f32[512]{0:T(512)S(1)} all-reduce(f32[512]{0:T(512)S(1)} %fusion.17), channel_id=1, replica_groups=mesh['macro'=8,'rep'=4] {'rep'}, use_global_device_ids=true, to_apply=%region_1.0 | all-reduce | flops 512 | bytes 4096 | tf_op jit(solution)/shard_map/psum | solution.py:113
  26.1 1.3 collective-permute-start.2
  27.4 5.2 %collective-permute-start.3 = (f32[1]{0:T(128)}, f32[1]{0:T(128)}, u32[]{:S(2)}, u32[]{:S(2)}) collective-permute-start(f32[1]{0:T(128)} %get-tuple-element.168), channel_id=1, source_target_pairs={{0,4},{4,8},{8,12},{12,16},{16,20},{20,24},{24,28},{1,5},{5,9},{9,... | collective-permute-start | bytes 20 | tf_op jit(solution)/shard_map/ppermute | solution.py:24
  40.8 5.9 %psum.78 = f32[512]{0:T(512)S(1)} all-reduce(f32[512]{0:T(512)S(1)} %fusion.35), channel_id=1, replica_groups=mesh['macro'=8,'rep'=4] {'rep'}, use_global_device_ids=true, to_apply=%region_3.0 | all-reduce | flops 512 | bytes 4096 | tf_op jit(solution)/shard_map/psum | solution.py:113
  47.4 25.6 %psum.79 = f32[]{:T(128)} all-reduce(f32[]{:T(128)} %multiply_reduce_fusion.14), channel_id=1, replica_groups=mesh['macro'=8,'rep'=4] {'macro'}, use_global_device_ids=true, to_apply=%region_5.0 | all-reduce | flops 1 | bytes 8 | tf_op jit(solution)/shard_map/psum | solution.py:117
  74.4 1.3 collective-permute-start.4
  75.7 5.1 %collective-permute-start.5 = (f32[1]{0:T(128)}, f32[1]{0:T(128)}, u32[]{:S(2)}, u32[]{:S(2)}) collective-permute-start(f32[1]{0:T(128)} %get-tuple-element.164), channel_id=1, source_target_pairs={{0,4},{4,8},{8,12},{12,16},{16,20},{20,24},{24,28},{1,5},{5,9},{9,... | collective-permute-start | bytes 20 | tf_op jit(solution)/shard_map/ppermute | solution.py:24
  89.0 5.7 %psum.80 = f32[512]{0:T(512)S(1)} all-reduce(f32[512]{0:T(512)S(1)} %fusion.53), channel_id=1, replica_groups=mesh['macro'=8,'rep'=4] {'rep'}, use_global_device_ids=true, to_apply=%region_7.0 | all-reduce | flops 512 | bytes 4096 | tf_op jit(solution)/shard_map/psum | solution.py:113
  95.4 1.4 pad_maximum_fusion.108
  96.8 19.5 %psum.81 = f32[2]{0:T(128)S(1)} all-reduce(f32[2]{0:T(128)S(1)} %pad_maximum_fusion.108), channel_id=1, replica_groups=mesh['macro'=8,'rep'=4] {'macro'}, use_global_device_ids=true, to_apply=%region_10.0 | all-reduce | flops 2 | bytes 16 | tf_op jit(solution)/shard_map/psum | solution.py:117
  122.3 1.3 collective-permute-start.6
  123.6 5.1 %collective-permute-start.7 = (f32[1]{0:T(128)}, f32[1]{0:T(128)}, u32[]{:S(2)}, u32[]{:S(2)}) collective-permute-start(f32[1]{0:T(128)} %get-tuple-element.160), channel_id=1, source_target_pairs={{0,4},{4,8},{8,12},{12,16},{16,20},{20,24},{24,28},{1,5},{5,9},{9,... | collective-permute-start | bytes 20 | tf_op jit(solution)/shard_map/ppermute | solution.py:24
  137.0 5.7 %psum.82 = f32[512]{0:T(512)S(1)} all-reduce(f32[512]{0:T(512)S(1)} %fusion.71), channel_id=1, replica_groups=mesh['macro'=8,'rep'=4] {'rep'}, use_global_device_ids=true, to_apply=%region_12.0 | all-reduce | flops 512 | bytes 4096 | tf_op jit(solution)/shard_map/psum | solution.py:113
  143.4 2.0 pad_maximum_fusion.109
  145.3 19.5 %psum.83 = f32[3]{0:T(128)S(1)} all-reduce(f32[3]{0:T(128)S(1)} %pad_maximum_fusion.109), channel_id=1, replica_groups=mesh['macro'=8,'rep'=4] {'macro'}, use_global_device_ids=true, to_apply=%region_16.0 | all-reduce | flops 3 | bytes 24 | tf_op jit(solution)/shard_map/psum | solution.py:117
  170.2 1.3 multiply_add_fusion.3
  172.2 1.3 collective-permute-start.8
  173.5 5.1 %collective-permute-start.9 = (f32[1]{0:T(128)}, f32[1]{0:T(128)}, u32[]{:S(2)}, u32[]{:S(2)}) collective-permute-start(f32[1]{0:T(128)} %get-tuple-element.156), channel_id=1, source_target_pairs={{0,4},{4,8},{8,12},{12,16},{16,20},{20,24},{24,28},{1,5},{5,9},{9,... | collective-permute-start | bytes 20 | tf_op jit(solution)/shard_map/ppermute | solution.py:24
  186.8 5.7 %psum.84 = f32[512]{0:T(512)S(1)} all-reduce(f32[512]{0:T(512)S(1)} %fusion.89), channel_id=1, replica_groups=mesh['macro'=8,'rep'=4] {'rep'}, use_global_device_ids=true, to_apply=%region_19.0 | all-reduce | flops 512 | bytes 4096 | tf_op jit(solution)/shard_map/psum | solution.py:113
  193.2 2.6 pad_maximum_fusion.110
  195.8 19.5 %psum.85 = f32[4]{0:T(128)S(1)} all-reduce(f32[4]{0:T(128)S(1)} %pad_maximum_fusion.110), channel_id=1, replica_groups=mesh['macro'=8,'rep'=4] {'macro'}, use_global_device_ids=true, to_apply=%region_24.0 | all-reduce | flops 4 | bytes 32 | tf_op jit(solution)/shard_map/psum | solution.py:117
  221.9 1.9 multiply_add_fusion.2
  224.4 1.3 collective-permute-start.10
  225.7 5.1 %collective-permute-start.11 = (f32[1]{0:T(128)}, f32[1]{0:T(128)}, u32[]{:S(2)}, u32[]{:S(2)}) collective-permute-start(f32[1]{0:T(128)} %get-tuple-element.152), channel_id=1, source_target_pairs={{0,4},{4,8},{8,12},{12,16},{16,20},{20,24},{24,28},{1,5},{5,9},{9,... | collective-permute-start | bytes 20 | tf_op jit(solution)/shard_map/ppermute | solution.py:24
  239.1 5.7 %psum.86 = f32[512]{0:T(512)S(1)} all-reduce(f32[512]{0:T(512)S(1)} %fusion.107), channel_id=1, replica_groups=mesh['macro'=8,'rep'=4] {'rep'}, use_global_device_ids=true, to_apply=%region_27.0 | all-reduce | flops 512 | bytes 4096 | tf_op jit(solution)/shard_map/psum | solution.py:113
  245.5 3.2 %stack.71 = f32[5]{0:T(128)S(1)} concatenate(f32[1]{0:T(128)} %bitcast.30, f32[1]{0:T(128)} %bitcast.31, f32[1]{0:T(128)} %bitcast.32, f32[1]{0:T(128)} %bitcast.33, f32[1]{0:T(128)} %bitcast.34), dimensions={0} | concatenate | bytes 40 | tf_op jit(solution)/shard_map/stack | solution.py:131
  248.7 19.5 %psum.87 = f32[5]{0:T(128)S(1)} all-reduce(f32[5]{0:T(128)S(1)} %stack.71), channel_id=1, replica_groups=mesh['macro'=8,'rep'=4] {'macro'}, use_global_device_ids=true, to_apply=%region_33.0 | all-reduce | flops 5 | bytes 40 | tf_op jit(solution)/shard_map/psum | solution.py:117
  (167 shorter events, 61.0 us)
Async XLA Ops:
  1.4 7.5 %copy-start.3 = (f32[512]{0:T(512)S(1)}, f32[512]{0:T(512)}, u32[]{:S(2)}) copy-start(f32[512]{0:T(512)} %param.5) | copy-start | bytes 6148
  1.4 7.5 %collective-permute-start = (f32[1]{0:T(128)}, f32[1]{0:T(128)}, u32[]{:S(2)}, u32[]{:S(2)}) collective-permute-start(f32[1]{0:T(128)} %get-tuple-element.171), channel_id=1, source_target_pairs={{4,0},{8,4},{12,8},{16,12},{20,16},{24,20},{28,24},{5,1},{9,5},{13... | collective-permute-start | bytes 20 | tf_op jit(solution)/shard_map/ppermute | solution.py:26
  2.8 6.8 %collective-permute-start.1 = (f32[1]{0:T(128)}, f32[1]{0:T(128)}, u32[]{:S(2)}, u32[]{:S(2)}) collective-permute-start(f32[1]{0:T(128)} %get-tuple-element.172), channel_id=1, source_target_pairs={{0,4},{4,8},{8,12},{12,16},{16,20},{20,24},{24,28},{1,5},{5,9},{9,... | collective-permute-start | bytes 20 | tf_op jit(solution)/shard_map/ppermute | solution.py:24
  8.9 0.8 copy-start.2
  12.5 1.0 copy-start
  12.9 0.7 copy-start.1
  26.1 6.5 %collective-permute-start.2 = (f32[1]{0:T(128)}, f32[1]{0:T(128)}, u32[]{:S(2)}, u32[]{:S(2)}) collective-permute-start(f32[1]{0:T(128)} %get-tuple-element.167), channel_id=1, source_target_pairs={{4,0},{8,4},{12,8},{16,12},{20,16},{24,20},{28,24},{5,1},{9,5},{13... | collective-permute-start | bytes 20 | tf_op jit(solution)/shard_map/ppermute | solution.py:26
  27.4 6.0 %collective-permute-start.3 = (f32[1]{0:T(128)}, f32[1]{0:T(128)}, u32[]{:S(2)}, u32[]{:S(2)}) collective-permute-start(f32[1]{0:T(128)} %get-tuple-element.168), channel_id=1, source_target_pairs={{0,4},{4,8},{8,12},{12,16},{16,20},{20,24},{24,28},{1,5},{5,9},{9,... | collective-permute-start | bytes 20 | tf_op jit(solution)/shard_map/ppermute | solution.py:24
  74.4 6.4 %collective-permute-start.4 = (f32[1]{0:T(128)}, f32[1]{0:T(128)}, u32[]{:S(2)}, u32[]{:S(2)}) collective-permute-start(f32[1]{0:T(128)} %get-tuple-element.163), channel_id=1, source_target_pairs={{4,0},{8,4},{12,8},{16,12},{20,16},{24,20},{28,24},{5,1},{9,5},{13... | collective-permute-start | bytes 20 | tf_op jit(solution)/shard_map/ppermute | solution.py:26
  75.7 5.9 %collective-permute-start.5 = (f32[1]{0:T(128)}, f32[1]{0:T(128)}, u32[]{:S(2)}, u32[]{:S(2)}) collective-permute-start(f32[1]{0:T(128)} %get-tuple-element.164), channel_id=1, source_target_pairs={{0,4},{4,8},{8,12},{12,16},{16,20},{20,24},{24,28},{1,5},{5,9},{9,... | collective-permute-start | bytes 20 | tf_op jit(solution)/shard_map/ppermute | solution.py:24
  122.3 6.4 %collective-permute-start.6 = (f32[1]{0:T(128)}, f32[1]{0:T(128)}, u32[]{:S(2)}, u32[]{:S(2)}) collective-permute-start(f32[1]{0:T(128)} %get-tuple-element.159), channel_id=1, source_target_pairs={{4,0},{8,4},{12,8},{16,12},{20,16},{24,20},{28,24},{5,1},{9,5},{13... | collective-permute-start | bytes 20 | tf_op jit(solution)/shard_map/ppermute | solution.py:26
  123.6 5.9 %collective-permute-start.7 = (f32[1]{0:T(128)}, f32[1]{0:T(128)}, u32[]{:S(2)}, u32[]{:S(2)}) collective-permute-start(f32[1]{0:T(128)} %get-tuple-element.160), channel_id=1, source_target_pairs={{0,4},{4,8},{8,12},{12,16},{16,20},{20,24},{24,28},{1,5},{5,9},{9,... | collective-permute-start | bytes 20 | tf_op jit(solution)/shard_map/ppermute | solution.py:24
  172.2 6.4 %collective-permute-start.8 = (f32[1]{0:T(128)}, f32[1]{0:T(128)}, u32[]{:S(2)}, u32[]{:S(2)}) collective-permute-start(f32[1]{0:T(128)} %get-tuple-element.155), channel_id=1, source_target_pairs={{4,0},{8,4},{12,8},{16,12},{20,16},{24,20},{28,24},{5,1},{9,5},{13... | collective-permute-start | bytes 20 | tf_op jit(solution)/shard_map/ppermute | solution.py:26
  173.5 5.9 %collective-permute-start.9 = (f32[1]{0:T(128)}, f32[1]{0:T(128)}, u32[]{:S(2)}, u32[]{:S(2)}) collective-permute-start(f32[1]{0:T(128)} %get-tuple-element.156), channel_id=1, source_target_pairs={{0,4},{4,8},{8,12},{12,16},{16,20},{20,24},{24,28},{1,5},{5,9},{9,... | collective-permute-start | bytes 20 | tf_op jit(solution)/shard_map/ppermute | solution.py:24
  224.4 6.4 %collective-permute-start.10 = (f32[1]{0:T(128)}, f32[1]{0:T(128)}, u32[]{:S(2)}, u32[]{:S(2)}) collective-permute-start(f32[1]{0:T(128)} %get-tuple-element.151), channel_id=1, source_target_pairs={{4,0},{8,4},{12,8},{16,12},{20,16},{24,20},{28,24},{5,1},{9,5},{13... | collective-permute-start | bytes 20 | tf_op jit(solution)/shard_map/ppermute | solution.py:26
  225.7 5.9 %collective-permute-start.11 = (f32[1]{0:T(128)}, f32[1]{0:T(128)}, u32[]{:S(2)}, u32[]{:S(2)}) collective-permute-start(f32[1]{0:T(128)} %get-tuple-element.152), channel_id=1, source_target_pairs={{0,4},{4,8},{8,12},{12,16},{16,20},{20,24},{24,28},{1,5},{5,9},{9,... | collective-permute-start | bytes 20 | tf_op jit(solution)/shard_map/ppermute | solution.py:24
where the time goes:
time: 278 us; the launch traced here: 277 us
  blocking collectives  139 us (50%)
  other arithmetic  49.8 us (18%)
  starting transfers between devices  39.4 us (14%)
  local copies, waits for them, and re-layouts  22.8 us (8%)
  between operations  21.2 us (8%)
  waiting for transfers between devices  4.81 us (2%)
    psum x5, blocking collectives, inner(): return lax.psum(values, 'macro')  104 us
    psum x6, blocking collectives, drift(): summed = lax.psum(increment_parts, 'rep')  35.1 us
    ppermute x6, starting transfers between devices, with_halo(): lax.ppermute(tail, axis, [(i, (i + 1) % count) for i in range(ends)])  31.6 us
    add x42, other arithmetic, ensemble_aggregate(): state + kappa * (upper + lower - 2.0 * state)  18.8 us
    slice x48, local copies, waits for them, and re-layouts, ensemble_aggregate(): lower = jnp.concatenate([left_col, state[:, :, :-1]], axis=2)  9.65 us
    ppermute x6, starting transfers between devices, with_halo(): lax.ppermute(head, axis, [((i + 1) % count, i) for i in range(ends)])  7.81 us
    concatenate x6, other arithmetic, with_halo(): jnp.concatenate([lax.ppermute(tail, axis, [(i, (i + 1) % count) for i in...  7.59 us
    another operation x3, other arithmetic, per_device(): dots = inner(jnp.stack(pieces))  5.98 us
  transfers between devices with their start and end apart: 12, of which 6 were waited for; matrix products, arithmetic and copies ran while one was open for 0% of the time, Pallas kernels for 0%

commit v1 on v0

--- a/solution.py
+++ b/solution.py
@@ -110,7 +110,9 @@
         increment_parts = ensemble_aggregate(
             padded_density, coarse_kinetic_speed, micro_spreading_coefficient, stochastic_kick
         )
-        summed = lax.psum(increment_parts, "rep")
+        summed = increment_parts
+        for hop in (1, 2):
+            summed = summed + lax.ppermute(summed, "rep", [(dev, dev ^ hop) for dev in range(4)])
         return summed * fluctuation_amplitude
 
     def inner(values):

time: 278 us -> 270 us (0.971)
  blocking collectives: 139 us -> 103 us
  waiting for transfers between devices: 4.81 us -> 21.8 us
  starting transfers between devices: 39.4 us -> 50.4 us
    psum x6 -> x0, blocking collectives: 35.1 us -> none  [drift(): summed = lax.psum(increment_parts, 'rep')]
    ppermute x0 -> x12, waiting for transfers between devices: none -> 16.7 us  [drift(): lax.ppermute(summed, 'rep', [(dev, dev ^ hop) for dev in range(4)])]
    ppermute x0 -> x12, starting transfers between devices: none -> 10.1 us  [drift(): lax.ppermute(summed, 'rep', [(dev, dev ^ hop) for dev in range(4)])]
  transfers between devices with their start and end apart: 12 -> 24, of which waited for: 6 -> 17; matrix products, arithmetic and copies ran while one was open for 0% -> 0% of each run, Pallas kernels for 0% -> 0%
where the time goes in v1:
time: 270 us; the launch traced here: 269 us
  blocking collectives  103 us (38%)
  starting transfers between devices  50.4 us (19%)
  other arithmetic  50.1 us (19%)
  local copies, waits for them, and re-layouts  22.5 us (8%)
  waiting for transfers between devices  21.8 us (8%)
  between operations  21.3 us (8%)
    psum x5, blocking collectives, inner(): return lax.psum(values, 'macro')  103 us
    ppermute x6, starting transfers between devices, with_halo(): lax.ppermute(tail, axis, [(i, (i + 1) % count) for i in range(ends)])  32.6 us
    add x42, other arithmetic, ensemble_aggregate(): state + kappa * (upper + lower - 2.0 * state)  18.7 us
    ppermute x12, waiting for transfers between devices, drift(): lax.ppermute(summed, 'rep', [(dev, dev ^ hop) for dev in range(4)])  16.7 us
    ppermute x12, starting transfers between devices, drift(): lax.ppermute(summed, 'rep', [(dev, dev ^ hop) for dev in range(4)])  10.1 us
    slice x48, local copies, waits for them, and re-layouts, ensemble_aggregate(): lower = jnp.concatenate([left_col, state[:, :, :-1]], axis=2)  9.65 us
    concatenate x6, other arithmetic, with_halo(): jnp.concatenate([lax.ppermute(tail, axis, [(i, (i + 1) % count) for i in...  7.98 us
    ppermute x6, starting transfers between devices, with_halo(): lax.ppermute(head, axis, [((i + 1) % count, i) for i in range(ends)])  7.81 us
  transfers between devices with their start and end apart: 24, of which 17 were waited for; matrix products, arithmetic and copies ran while one was open for 0% of the time, Pallas kernels for 0%

profile of v1, /device:TPU:0, one launch (start us, length us, event | category | flops | bytes accessed | tf_op | source)
XLA Modules:
  0.0 269.0 jit_solution(8321448398449658509)
XLA Ops:
  0.0 1.4 fusion.354
  1.4 1.4 collective-permute-start
  2.8 6.1 %collective-permute-start.1 = (f32[1]{0:T(128)}, f32[1]{0:T(128)}, u32[]{:S(2)}, u32[]{:S(2)}) collective-permute-start(f32[1]{0:T(128)} %get-tuple-element.175), channel_id=1, source_target_pairs={{0,4},{4,8},{8,12},{12,16},{16,20},{20,24},{24,28},{1,5},{5,9},{9,... | collective-permute-start | bytes 20 | tf_op jit(solution)/shard_map/ppermute | solution.py:24
  9.8 1.3 pad_maximum_fusion.96
  20.3 2.0 collective-permute-start.3
  22.4 1.6 collective-permute-done.3
  25.8 6.0 %collective-permute-start.5 = (f32[1]{0:T(128)}, f32[1]{0:T(128)}, u32[]{:S(2)}, u32[]{:S(2)}) collective-permute-start(f32[1]{0:T(128)} %get-tuple-element.171), channel_id=1, source_target_pairs={{0,4},{4,8},{8,12},{12,16},{16,20},{20,24},{24,28},{1,5},{5,9},{9,... | collective-permute-start | bytes 20 | tf_op jit(solution)/shard_map/ppermute | solution.py:24
  32.7 1.3 pad_maximum_fusion.98
  41.5 1.5 collective-permute-start.7
  43.0 2.1 collective-permute-done.7
  45.7 25.6 %psum.35 = f32[]{:T(128)} all-reduce(f32[]{:T(128)} %get-tuple-element.30), channel_id=1, replica_groups=mesh['macro'=8,'rep'=4] {'macro'}, use_global_device_ids=true, to_apply=%region_3.0 | all-reduce | flops 1 | bytes 8 | tf_op jit(solution)/shard_map/psum | solution.py:119
  73.9 5.1 %collective-permute-start.9 = (f32[1]{0:T(128)}, f32[1]{0:T(128)}, u32[]{:S(2)}, u32[]{:S(2)}) collective-permute-start(f32[1]{0:T(128)} %get-tuple-element.167), channel_id=1, source_target_pairs={{0,4},{4,8},{8,12},{12,16},{16,20},{20,24},{24,28},{1,5},{5,9},{9,... | collective-permute-start | bytes 20 | tf_op jit(solution)/shard_map/ppermute | solution.py:24
  88.7 1.5 collective-permute-start.11
  90.3 2.1 collective-permute-done.11
  93.0 1.3 pad_maximum_fusion.108
  94.3 19.3 %psum.36 = f32[2]{0:T(128)S(1)} all-reduce(f32[2]{0:T(128)S(1)} %pad_maximum_fusion.108), channel_id=1, replica_groups=mesh['macro'=8,'rep'=4] {'macro'}, use_global_device_ids=true, to_apply=%region_7.0 | all-reduce | flops 2 | bytes 16 | tf_op jit(solution)/shard_map/psum | solution.py:119
  118.8 5.1 %collective-permute-start.13 = (f32[1]{0:T(128)}, f32[1]{0:T(128)}, u32[]{:S(2)}, u32[]{:S(2)}) collective-permute-start(f32[1]{0:T(128)} %get-tuple-element.163), channel_id=1, source_target_pairs={{0,4},{4,8},{8,12},{12,16},{16,20},{20,24},{24,28},{1,5},{5,9},{9,... | collective-permute-start | bytes 20 | tf_op jit(solution)/shard_map/ppermute | solution.py:24
  124.7 1.4 pad_maximum_fusion.102
  133.5 1.5 collective-permute-start.15
  135.0 2.1 collective-permute-done.15
  137.8 1.9 pad_maximum_fusion.109
  139.7 19.3 %psum.37 = f32[3]{0:T(128)S(1)} all-reduce(f32[3]{0:T(128)S(1)} %pad_maximum_fusion.109), channel_id=1, replica_groups=mesh['macro'=8,'rep'=4] {'macro'}, use_global_device_ids=true, to_apply=%region_12.0 | all-reduce | flops 3 | bytes 24 | tf_op jit(solution)/shard_map/psum | solution.py:119
  165.0 5.1 %collective-permute-start.17 = (f32[1]{0:T(128)}, f32[1]{0:T(128)}, u32[]{:S(2)}, u32[]{:S(2)}) collective-permute-start(f32[1]{0:T(128)} %get-tuple-element.159), channel_id=1, source_target_pairs={{0,4},{4,8},{8,12},{12,16},{16,20},{20,24},{24,28},{1,5},{5,9},{9,... | collective-permute-start | bytes 20 | tf_op jit(solution)/shard_map/ppermute | solution.py:24
  179.6 1.5 collective-permute-start.19
  181.1 2.1 collective-permute-done.19
  183.9 2.6 pad_maximum_fusion.110
  186.5 19.3 %psum.38 = f32[4]{0:T(128)S(1)} all-reduce(f32[4]{0:T(128)S(1)} %pad_maximum_fusion.110), channel_id=1, replica_groups=mesh['macro'=8,'rep'=4] {'macro'}, use_global_device_ids=true, to_apply=%region_19.0 | all-reduce | flops 4 | bytes 32 | tf_op jit(solution)/shard_map/psum | solution.py:119
  208.6 1.9 multiply_add_fusion.2
  212.5 5.1 %collective-permute-start.21 = (f32[1]{0:T(128)}, f32[1]{0:T(128)}, u32[]{:S(2)}, u32[]{:S(2)}) collective-permute-start(f32[1]{0:T(128)} %get-tuple-element.155), channel_id=1, source_target_pairs={{0,4},{4,8},{8,12},{12,16},{16,20},{20,24},{24,28},{1,5},{5,9},{9,... | collective-permute-start | bytes 20 | tf_op jit(solution)/shard_map/ppermute | solution.py:24
  227.1 1.5 collective-permute-start.23
  237.9 3.2 %stack.71 = f32[5]{0:T(128)S(1)} concatenate(f32[1]{0:T(128)} %bitcast.30, f32[1]{0:T(128)} %bitcast.31, f32[1]{0:T(128)} %bitcast.32, f32[1]{0:T(128)} %bitcast.33, f32[1]{0:T(128)} %bitcast.34), dimensions={0} | concatenate | bytes 40 | tf_op jit(solution)/shard_map/stack | solution.py:133
  241.2 19.3 %psum.39 = f32[5]{0:T(128)S(1)} all-reduce(f32[5]{0:T(128)S(1)} %stack.71), channel_id=1, replica_groups=mesh['macro'=8,'rep'=4] {'macro'}, use_global_device_ids=true, to_apply=%region_27.0 | all-reduce | flops 5 | bytes 40 | tf_op jit(solution)/shard_map/psum | solution.py:119
  (191 shorter events, 74.9 us)
Async XLA Ops:
  1.4 7.5 %copy-start.3 = (f32[512]{0:T(512)S(1)}, f32[512]{0:T(512)}, u32[]{:S(2)}) copy-start(f32[512]{0:T(512)} %param.5) | copy-start | bytes 6148
  1.4 7.5 %collective-permute-start = (f32[1]{0:T(128)}, f32[1]{0:T(128)}, u32[]{:S(2)}, u32[]{:S(2)}) collective-permute-start(f32[1]{0:T(128)} %get-tuple-element.174), channel_id=1, source_target_pairs={{4,0},{8,4},{12,8},{16,12},{20,16},{24,20},{28,24},{5,1},{9,5},{13... | collective-permute-start | bytes 20 | tf_op jit(solution)/shard_map/ppermute | solution.py:26
  2.8 7.0 %collective-permute-start.1 = (f32[1]{0:T(128)}, f32[1]{0:T(128)}, u32[]{:S(2)}, u32[]{:S(2)}) collective-permute-start(f32[1]{0:T(128)} %get-tuple-element.175), channel_id=1, source_target_pairs={{0,4},{4,8},{8,12},{12,16},{16,20},{20,24},{24,28},{1,5},{5,9},{9,... | collective-permute-start | bytes 20 | tf_op jit(solution)/shard_map/ppermute | solution.py:24
  8.9 0.9 copy-start.2
  12.7 1.0 copy-start
  13.0 0.7 copy-start.1
  19.1 1.2 collective-permute-start.2
  20.3 3.6 %collective-permute-start.3 = (f32[512]{0:T(512)S(1)}, f32[512]{0:T(512)S(1)}, u32[]{:S(2)}, u32[]{:S(2)}) collective-permute-start(f32[512]{0:T(512)S(1)} %add.1256), channel_id=1, source_target_pairs={{0,2},{1,3},{2,0},{3,1},{4,6},{5,7},{6,4},{7,5},{8,10},{9,11},{10,... | collective-permute-start | bytes 6152 | tf_op jit(solution)/shard_map/ppermute | solution.py:115
  24.5 7.3 %collective-permute-start.4 = (f32[1]{0:T(128)}, f32[1]{0:T(128)}, u32[]{:S(2)}, u32[]{:S(2)}) collective-permute-start(f32[1]{0:T(128)} %get-tuple-element.170), channel_id=1, source_target_pairs={{4,0},{8,4},{12,8},{16,12},{20,16},{24,20},{28,24},{5,1},{9,5},{13... | collective-permute-start | bytes 20 | tf_op jit(solution)/shard_map/ppermute | solution.py:26
  25.8 6.9 %collective-permute-start.5 = (f32[1]{0:T(128)}, f32[1]{0:T(128)}, u32[]{:S(2)}, u32[]{:S(2)}) collective-permute-start(f32[1]{0:T(128)} %get-tuple-element.171), channel_id=1, source_target_pairs={{0,4},{4,8},{8,12},{12,16},{16,20},{20,24},{24,28},{1,5},{5,9},{9,... | collective-permute-start | bytes 20 | tf_op jit(solution)/shard_map/ppermute | solution.py:24
  40.3 1.2 collective-permute-start.6
  41.5 3.6 %collective-permute-start.7 = (f32[512]{0:T(512)S(1)}, f32[512]{0:T(512)S(1)}, u32[]{:S(2)}, u32[]{:S(2)}) collective-permute-start(f32[512]{0:T(512)S(1)} %add.1291), channel_id=1, source_target_pairs={{0,2},{1,3},{2,0},{3,1},{4,6},{5,7},{6,4},{7,5},{8,10},{9,11},{10,... | collective-permute-start | bytes 6152 | tf_op jit(solution)/shard_map/ppermute | solution.py:115
  72.6 6.4 %collective-permute-start.8 = (f32[1]{0:T(128)}, f32[1]{0:T(128)}, u32[]{:S(2)}, u32[]{:S(2)}) collective-permute-start(f32[1]{0:T(128)} %get-tuple-element.166), channel_id=1, source_target_pairs={{4,0},{8,4},{12,8},{16,12},{20,16},{24,20},{28,24},{5,1},{9,5},{13... | collective-permute-start | bytes 20 | tf_op jit(solution)/shard_map/ppermute | solution.py:26
  73.9 6.0 %collective-permute-start.9 = (f32[1]{0:T(128)}, f32[1]{0:T(128)}, u32[]{:S(2)}, u32[]{:S(2)}) collective-permute-start(f32[1]{0:T(128)} %get-tuple-element.167), channel_id=1, source_target_pairs={{0,4},{4,8},{8,12},{12,16},{16,20},{20,24},{24,28},{1,5},{5,9},{9,... | collective-permute-start | bytes 20 | tf_op jit(solution)/shard_map/ppermute | solution.py:24
  87.5 1.2 collective-permute-start.10
  88.7 3.6 %collective-permute-start.11 = (f32[512]{0:T(512)S(1)}, f32[512]{0:T(512)S(1)}, u32[]{:S(2)}, u32[]{:S(2)}) collective-permute-start(f32[512]{0:T(512)S(1)} %add.1326), channel_id=1, source_target_pairs={{0,2},{1,3},{2,0},{3,1},{4,6},{5,7},{6,4},{7,5},{8,10},{9,11},{10,... | collective-permute-start | bytes 6152 | tf_op jit(solution)/shard_map/ppermute | solution.py:115
  117.5 6.4 %collective-permute-start.12 = (f32[1]{0:T(128)}, f32[1]{0:T(128)}, u32[]{:S(2)}, u32[]{:S(2)}) collective-permute-start(f32[1]{0:T(128)} %get-tuple-element.162), channel_id=1, source_target_pairs={{4,0},{8,4},{12,8},{16,12},{20,16},{24,20},{28,24},{5,1},{9,5},{13... | collective-permute-start | bytes 20 | tf_op jit(solution)/shard_map/ppermute | solution.py:26
  118.8 5.9 %collective-permute-start.13 = (f32[1]{0:T(128)}, f32[1]{0:T(128)}, u32[]{:S(2)}, u32[]{:S(2)}) collective-permute-start(f32[1]{0:T(128)} %get-tuple-element.163), channel_id=1, source_target_pairs={{0,4},{4,8},{8,12},{12,16},{16,20},{20,24},{24,28},{1,5},{5,9},{9,... | collective-permute-start | bytes 20 | tf_op jit(solution)/shard_map/ppermute | solution.py:24
  132.3 1.2 collective-permute-start.14
  133.5 3.6 %collective-permute-start.15 = (f32[512]{0:T(512)S(1)}, f32[512]{0:T(512)S(1)}, u32[]{:S(2)}, u32[]{:S(2)}) collective-permute-start(f32[512]{0:T(512)S(1)} %add.1362), channel_id=1, source_target_pairs={{0,2},{1,3},{2,0},{3,1},{4,6},{5,7},{6,4},{7,5},{8,10},{9,11},{10,... | collective-permute-start | bytes 6152 | tf_op jit(solution)/shard_map/ppermute | solution.py:115
  163.7 6.4 %collective-permute-start.16 = (f32[1]{0:T(128)}, f32[1]{0:T(128)}, u32[]{:S(2)}, u32[]{:S(2)}) collective-permute-start(f32[1]{0:T(128)} %get-tuple-element.158), channel_id=1, source_target_pairs={{4,0},{8,4},{12,8},{16,12},{20,16},{24,20},{28,24},{5,1},{9,5},{13... | collective-permute-start | bytes 20 | tf_op jit(solution)/shard_map/ppermute | solution.py:26
  165.0 5.9 %collective-permute-start.17 = (f32[1]{0:T(128)}, f32[1]{0:T(128)}, u32[]{:S(2)}, u32[]{:S(2)}) collective-permute-start(f32[1]{0:T(128)} %get-tuple-element.159), channel_id=1, source_target_pairs={{0,4},{4,8},{8,12},{12,16},{16,20},{20,24},{24,28},{1,5},{5,9},{9,... | collective-permute-start | bytes 20 | tf_op jit(solution)/shard_map/ppermute | solution.py:24
  178.4 1.2 collective-permute-start.18
  179.6 3.6 %collective-permute-start.19 = (f32[512]{0:T(512)S(1)}, f32[512]{0:T(512)S(1)}, u32[]{:S(2)}, u32[]{:S(2)}) collective-permute-start(f32[512]{0:T(512)S(1)} %add.1400), channel_id=1, source_target_pairs={{0,2},{1,3},{2,0},{3,1},{4,6},{5,7},{6,4},{7,5},{8,10},{9,11},{10,... | collective-permute-start | bytes 6152 | tf_op jit(solution)/shard_map/ppermute | solution.py:115
  211.2 6.4 %collective-permute-start.20 = (f32[1]{0:T(128)}, f32[1]{0:T(128)}, u32[]{:S(2)}, u32[]{:S(2)}) collective-permute-start(f32[1]{0:T(128)} %get-tuple-element.154), channel_id=1, source_target_pairs={{4,0},{8,4},{12,8},{16,12},{20,16},{24,20},{28,24},{5,1},{9,5},{13... | collective-permute-start | bytes 20 | tf_op jit(solution)/shard_map/ppermute | solution.py:26
  212.5 5.9 %collective-permute-start.21 = (f32[1]{0:T(128)}, f32[1]{0:T(128)}, u32[]{:S(2)}, u32[]{:S(2)}) collective-permute-start(f32[1]{0:T(128)} %get-tuple-element.155), channel_id=1, source_target_pairs={{0,4},{4,8},{8,12},{12,16},{16,20},{20,24},{24,28},{1,5},{5,9},{9,... | collective-permute-start | bytes 20 | tf_op jit(solution)/shard_map/ppermute | solution.py:24
  225.9 1.2 collective-permute-start.22
  227.1 10.1 %collective-permute-start.23 = (f32[512]{0:T(512)S(1)}, f32[512]{0:T(512)S(1)}, u32[]{:S(2)}, u32[]{:S(2)}) collective-permute-start(f32[512]{0:T(512)S(1)} %add.1439), channel_id=1, source_target_pairs={{0,2},{1,3},{2,0},{3,1},{4,6},{5,7},{6,4},{7,5},{8,10},{9,11},{10,... | collective-permute-start | bytes 6152 | tf_op jit(solution)/shard_map/ppermute | solution.py:115
